TPU v7x, 32 devices: a whole 2x2x4 slice. The times are simulated.
32 devices in a mesh: row: 8 (over z, x), col: 2 (over y), depth: 2 (over core).
Axes of the slice: x: 2, y: 2, z: 4, core: 2. Of those that a mesh axis runs over, the one named last changes fastest.
Arguments:
- tokens: bfloat16 [1024, 5376], P('row', 'depth'), may hold values from -6 to 6
- gate_weight: bfloat16 [9216, 5376], P(('col', 'row'), 'depth'), may hold values from -0.078125 to 0.078125
- up_weight: bfloat16 [9216, 5376], P(('col', 'row'), 'depth'), may hold values from -0.078125 to 0.078125
- down_weight: bfloat16 [9216, 5376], P(('col', 'depth'), 'row'), may hold values from -0.09375 to 0.09375
Outputs:
- output: bfloat16 [1024, 5376], P('row', ('col', 'depth'))
All inputs are finite; a program needn't handle non-finite values.
Results may differ from a plain program's by a relative error of at most 0.0049.
Values may be sent and summed in bfloat16 or wider, within the bound.
A program may use at most 128 MiB of HBM per device.

v0:
```python
import functools

import jax
import jax.numpy as jnp
from jax import lax
from jax.experimental import pallas as pl
from jax.experimental.pallas import tpu as pltpu
from jax.sharding import PartitionSpec as P

MESH = pl.DeviceIdType.MESH
F32 = jnp.float32
BF16 = jnp.bfloat16


def row_at(place, n):
    back = place // (n // 2)
    return 2 * place * (1 - back) + (2 * (n - 1 - place) + 1) * back


def kernel(n, tok_hbm, gate_hbm, up_hbm, down_hbm, out_ref, tok, weights, turned, rows_of, down, part, theirs, hid,
           total, other, send_y, from_y, load_sem, down_load, down_send, down_recv, tok_send, tok_recv,
           y_send, y_recv, part_send, part_recv, hid_send, hid_recv, sum_send, sum_recv, col_send, col_recv,
           done, land, passed, out_send, out_recv, pass_send, pass_recv):
    row, col, core = lax.axis_index("row"), lax.axis_index("col"), lax.axis_index("depth")
    half = n // 2
    x, z = row % 2, row // 2
    place = z * (1 - x) + (n - 1 - z) * x
    ways = ({"row": row_at((place + 1) % n, n)}, {"row": row_at((place + n - 1) % n, n)})
    beside, partner = {"col": 1 - col}, {"depth": 1 - core}
    block = tok_hbm.shape[0]
    third = tok_hbm.shape[1] // 3
    units = gate_hbm.shape[0]
    share = units // 2

    def remote(src, dst, send, recv, to):
        return pltpu.make_async_remote_copy(src_ref=src, dst_ref=dst, send_sem=send, recv_sem=recv,
                                            device_id=to, device_id_type=MESH)

    loads = [pltpu.make_async_copy(tok_hbm.at[:, pl.ds(t * third, third)], tok.at[t, 0], load_sem.at[t])
             for t in range(3)]
    loads += [pltpu.make_async_copy(gate_hbm, weights.at[0], load_sem.at[3]),
              pltpu.make_async_copy(up_hbm, weights.at[1], load_sem.at[4]),
              pltpu.make_async_copy(down_hbm, turned, load_sem.at[5])]
    for copy in loads:
        copy.start()
    barrier = pltpu.get_barrier_semaphore()
    for peer in ways + (beside, partner):
        pl.semaphore_signal(barrier, inc=1, device_id=peer, device_id_type=MESH)
    near = 1 - jnp.minimum((z // 2 - core) * (z // 2 - core) + (z % 2 - core) * (z % 2 - core), 1)
    sinks = [{"row": 4 * core + m, "depth": z % 2} for m in range(4)]
    feeds = [{"row": 4 * (m // 2) + 2 * core + m % 2, "depth": z // 2} for m in range(4)]
    away = [(row - peer["row"]) * (row - peer["row"]) + (core - peer["depth"]) * (core - peer["depth"])
            for peer in sinks + feeds]
    for peer, far in zip(sinks + feeds, away):
        @pl.when(far > 0)
        def _(peer=peer):
            pl.semaphore_signal(barrier, inc=1, device_id=peer, device_id_type=MESH)
    pl.semaphore_wait(barrier, 12 - 2 * near)
    for copy in loads[:3]:
        copy.wait()

    def slot(hop, way):
        return 0 if hop == 0 else 1 if hop == half else 2 * hop + way

    def rounds(hop, chunk):
        return (chunk,) if hop == half else (0, 1)

    started = []

    def go(copy):
        copy.start()
        started.append(copy)

    def tok_copy(hop, way, chunk):
        t = 2 * col if chunk == 0 else 1
        return remote(tok.at[t, slot(hop - 1, way)], tok.at[t, slot(hop, way)],
                      tok_send.at[way, hop - 1, chunk], tok_recv.at[way, hop - 1, chunk], ways[way])

    def y_copy(at, t):
        return remote(tok.at[t, at], tok.at[t, at], y_send.at[at], y_recv.at[at], beside)

    for chunk in (0, 1):
        for way in (0, 1):
            go(tok_copy(1, way, chunk))

    local_down, remote_down = [], []
    for i in range(half):
        keep = rows_of.at[pl.ds(i * units + core * share, share)]
        give = rows_of.at[pl.ds(i * units + (1 - core) * share, share)]
        dst = down.at[core * half + i]
        local_down.append(pltpu.make_async_copy(keep, dst, down_load.at[i]))
        remote_down.append(remote(give, dst, down_send.at[i], down_recv.at[i], partner))
    for copy in loads[3:]:
        copy.wait()

    @pl.loop(0, turned.shape[1] // 128)
    def _(step):
        at = pl.ds(pl.multiple_of(step * 128, 128), 128)
        rows_of[at, :] = turned[:, at].T

    for copy in local_down + remote_down:
        copy.start()

    def gate_up(group, slots, to):
        wide = block * len(slots)
        first = slots[0]

        @pl.loop(0, 4)
        def _(step):
            side, kind = step // 2, step % 2
            which = (1 - core) * (1 - side) + core * side
            rows = pl.ds(pl.multiple_of(which * share, 16), share)
            acc = None
            for t in range(3):
                seen = tok[t, first:first + len(slots)].reshape(wide, third)
                term = lax.dot_general(weights[kind, rows, t * third:(t + 1) * third], seen,
                                       (((1,), (1,)), ((), ())), preferred_element_type=F32)
                acc = term if acc is None else acc + term
            part[group, side, kind, :, :wide] = acc

        swap = remote(part.at[group, 0, :, :, pl.ds(0, wide)], theirs.at[group, :, :, pl.ds(0, wide)],
                      part_send.at[group], part_recv.at[group], partner)
        go(swap)
        swap.wait_recv()
        gate = part[group, 1, 0, :, :wide] + theirs[group, 0, :, :wide]
        up = part[group, 1, 1, :, :wide] + theirs[group, 1, :, :wide]
        hid[0, :, to:to + wide] = (gate / (1.0 + jnp.exp(-gate)) * up).astype(BF16)

    wide_piece = 2 * block

    def hid_copy(piece, hop, way):
        at = pl.ds((piece - 1) * wide_piece, wide_piece)
        return remote(hid.at[slot(hop - 1, way), :, at], hid.at[slot(hop, way), :, at],
                      hid_send.at[way, hop - 1, piece - 1], hid_recv.at[way, hop - 1, piece - 1], ways[way])

    def hid_rounds(piece, hop):
        return (piece % 2,) if hop == half else (0, 1)

    def add_down(at, source, piece):
        lanes = slice((piece - 1) * wide_piece, piece * wide_piece)
        term = lax.dot_general(hid[at, :, lanes], down[row_at(source, n)], (((0,), (0,)), ((), ())),
                               preferred_element_type=F32)
        before = source if piece == half else (source + n - piece) % n
        for k, token_block in enumerate((before, (source + piece) % n)):
            total[row_at(token_block, n)] += term[k * block:(k + 1) * block]

    def wave(number):
        for piece in range(1, half + 1):
            hop = number + 1 - piece
            if hop == 1:
                for way in (0, 1):
                    go(hid_copy(piece, 1, way))
            elif 2 <= hop <= half + 1:
                for way in hid_rounds(piece, hop - 1):
                    hid_copy(piece, hop - 1, way).wait_recv()
                    if hop <= half and way in hid_rounds(piece, hop):
                        go(hid_copy(piece, hop, way))
        for piece in range(1, half + 1):
            hop = number - piece
            if hop == 0:
                add_down(0, place, piece)
            elif hop == half:
                add_down(1, (place + half) % n, piece)
            elif 1 <= hop < half:
                @pl.loop(0, 2)
                def _(way):
                    add_down(2 * hop + way, (place + n - hop + 2 * hop * way) % n, piece)

    total[...] = jnp.zeros_like(total)
    for hop in range(1, half + 1):
        for chunk in (0, 1):
            for way in rounds(hop, chunk):
                tok_copy(hop, way, chunk).wait_recv()
                if hop < half and way in rounds(hop + 1, chunk):
                    go(tok_copy(hop + 1, way, chunk))
                if chunk == 0:
                    go(y_copy(slot(hop, way), 2 * col))
        if hop == 1:
            gate_up(0, [0], (half - 1) * wide_piece)
            for copy in local_down:
                copy.wait()
            for copy in remote_down:
                copy.wait()
        else:
            slots = [2 * (hop - 1), 2 * (hop - 1) + 1]
            for at in slots:
                y_copy(at, 2 - 2 * col).wait_recv()
            gate_up(hop - 1, slots, (hop - 2) * wide_piece)
            wave(hop - 1)
    y_copy(1, 2 - 2 * col).wait_recv()
    gate_up(half, [1], (half - 1) * wide_piece + block)
    for number in range(half, 2 * half + 1):
        wave(number)

    part_rows = block // 2

    def rows_in(c):
        return pl.ds(pl.multiple_of(c * part_rows, part_rows), part_rows)

    def sum_copy(side, m):
        c = 1 - col if side == 0 else col
        return remote(total.at[4 * (1 - core) + m, rows_in(c)], other.at[side, m],
                      sum_send.at[side, m], sum_recv.at[side, m], partner)

    def col_copy(m):
        return remote(send_y.at[m], from_y.at[m], col_send.at[m], col_recv.at[m], beside)

    spot = z // 2 * 2 + x

    def out_copy(m):
        return remote(done.at[m], land.at[spot], out_send.at[m], out_recv.at[spot], sinks[m])

    def landed(at):
        remote(done.at[0], land.at[at], out_send.at[0], out_recv.at[at], beside).wait_recv()

    def pass_copy(k):
        return remote(land.at[(1 - col) * 2 + k], passed.at[k], pass_send.at[k], pass_recv.at[k], beside)

    for side in (0, 1):
        for m in range(4):
            go(sum_copy(side, m))
    for m in range(4):
        sum_copy(0, m).wait_recv()
        send_y[m] = (total[4 * core + m, rows_in(1 - col)] + other[0, m]).astype(BF16)
        go(col_copy(m))
    for m in range(4):
        sum_copy(1, m).wait_recv()
        mine = total[4 * core + m, rows_in(col)] + other[1, m]
        col_copy(m).wait_recv()
        done[m] = (mine + from_y[m].astype(F32)).astype(BF16)

        @pl.when(away[m] > 0)
        def _():
            out_copy(m).start()

        @pl.when(away[m] == 0)
        def _():
            pltpu.make_async_copy(done.at[m], land.at[spot], out_recv.at[spot]).start()
    for k in (0, 1):
        landed((1 - col) * 2 + k)
        go(pass_copy(k))
    for k in (0, 1):
        landed(col * 2 + k)
        out_ref[k, rows_in(col)] = land[col * 2 + k]
    for k in (0, 1):
        pass_copy(k).wait_recv()
        out_ref[k, rows_in(1 - col)] = passed[k]
    for m in range(4):
        @pl.when(away[m] > 0)
        def _():
            out_copy(m).wait_send()
    for copy in started:
        copy.wait_send()


def partial_sums(n, tokens, gate_weight, up_weight, down_weight):
    block, width = tokens.shape
    units = gate_weight.shape[0]
    features = down_weight.shape[1]
    piece = block // 2
    half, share = n // 2, units // 2
    every = n * block
    dma = pltpu.SemaphoreType.DMA
    return pl.pallas_call(
        functools.partial(kernel, n),
        out_shape=jax.ShapeDtypeStruct((2, block, features), BF16),
        in_specs=[pl.BlockSpec(memory_space=pl.ANY)] * 4,
        out_specs=pl.BlockSpec(memory_space=pltpu.VMEM),
        scratch_shapes=[
            pltpu.VMEM((3, n, block, width // 3), BF16),
            pltpu.VMEM((2, units, width), BF16),
            pltpu.VMEM((features, down_weight.shape[0]), BF16),
            pltpu.VMEM((down_weight.shape[0], features), BF16),
            pltpu.VMEM((n, share, features), BF16),
            pltpu.VMEM((half + 1, 2, 2, share, 2 * block), F32),
            pltpu.VMEM((half + 1, 2, share, 2 * block), F32),
            pltpu.VMEM((n, share, every), BF16),
            pltpu.VMEM((n, block, features), F32),
            pltpu.VMEM((2, 4, piece, features), F32),
            pltpu.VMEM((4, piece, features), BF16),
            pltpu.VMEM((4, piece, features), BF16),
            dma((6,)),
            dma((half,)), dma((half,)), dma((half,)),
            dma((2, half, 2)), dma((2, half, 2)),
            dma((n,)), dma((n,)),
            dma((half + 1,)), dma((half + 1,)),
            dma((2, half, half)), dma((2, half, half)),
            dma((2, 4)), dma((2, 4)),
            dma((4,)), dma((4,)),
            pltpu.VMEM((4, piece, features), BF16),
            pltpu.VMEM((4, piece, features), BF16),
            pltpu.VMEM((2, piece, features), BF16),
            dma((4,)), dma((4,)), dma((2,)), dma((2,)),
        ],
        compiler_params=pltpu.CompilerParams(
            collective_id=0, has_side_effects=True, vmem_limit_bytes=60 * 1024 * 1024
        ),
    )(tokens, gate_weight, up_weight, down_weight.T)


def send_out(mine, rows, cols, depths):
    quarters = cols * depths
    per = rows // quarters
    block = mine.shape[0] // per
    width = mine.shape[1]
    row = lax.axis_index("row")
    low = row % per
    got = jnp.zeros((block, per, width), jnp.bfloat16)
    for k in range(per):
        pairs = []
        for r in range(rows):
            for q in range(quarters):
                a, e = r // per, r % per
                to_row = q * per + (e + k) % per
                pairs.append((r * quarters + q, to_row * quarters + a))
        piece = lax.dynamic_slice_in_dim(mine, (low + k) % per * block, block, 0)
        piece = lax.ppermute(piece, ("row", "col", "depth"), pairs)
        got = lax.dynamic_update_slice_in_dim(got, piece[:, None], (low - k) % per, 1)
    return got.reshape(block, per * width)


def solution(mesh):
    rows, cols, depths = (mesh.shape[a] for a in ("row", "col", "depth"))

    def local(tokens, gate_weight, up_weight, down_weight):
        units = gate_weight.shape[0]
        every = lax.all_gather(tokens, "row", axis=0, tiled=True)
        down = down_weight.reshape(rows // depths, depths, units // depths, -1)
        down = lax.all_to_all(down, "depth", split_axis=1, concat_axis=0, tiled=True)
        down = down.reshape(rows, units // depths, -1)
        paired = jnp.stack([gate_weight, up_weight])
        sums = jnp.einsum("td,gfd->gtf", every, paired, preferred_element_type=jnp.float32)
        sums = lax.psum_scatter(sums, "depth", scatter_dimension=2, tiled=True)
        hidden = (jax.nn.silu(sums[0]) * sums[1]).astype(jnp.bfloat16)
        hidden = lax.all_gather(hidden, "row", axis=0)
        partial = jnp.einsum("rtk,rkc->tc", hidden, down, preferred_element_type=jnp.float32)
        mine = lax.psum_scatter(partial, ("col", "depth"), scatter_dimension=0, tiled=True)
        return send_out(mine.astype(BF16), rows, cols, depths)

    def fused(*args):
        return jnp.concatenate(list(partial_sums(rows, *args)), axis=1)

    in_specs = (
        P("row", "depth"),
        P(("col", "row"), "depth"),
        P(("col", "row"), "depth"),
        P(("col", "depth"), "row"),
    )
    out_specs = P("row", ("col", "depth"))
    small = cols == 2 and depths == 2 and rows == 8
    return jax.shard_map(fused if small else local, mesh=mesh, in_specs=in_specs, out_specs=out_specs, check_vma=False)
```

profile of v0, /device:TPU:0, one launch (start us, length us, event | category | flops | bytes accessed | tf_op | source)
XLA Modules:
  0.0 111.8 jit_solution(17394847550342655836)
XLA Ops:
  0.0 109.7 %shard_map.46 = bf16[2,128,672]{2,1,0:T(8,128)(2,1)} custom-call(bf16[128,2688]{1,0:T(8,128)(2,1)} %tok_hbm.1, bf16[576,2688]{1,0:T(8,128)(2,1)} %gate_hbm.1, bf16[576,2688]{1,0:T(8,128)(2,1)} %up_hbm.1, bf16[672,2304]{1,0:T(8,128)(2,1)} %bitcast.5), custom_call_target="tpu_custom_call" | custom-call | tf_op jit(solution)/shard_map/pallas_call | solution.py:264
  109.7 1.0 slice_bitcast_fusion.1
  110.8 0.1 pad_maximum_fusion
  110.9 0.9 copy.5
where the time goes:
time: 113 us; the launch traced here: 112 us
  Pallas kernels  110 us (97%)
  local copies, waits for them, and re-layouts  1.96 us (2%)
    pallas_call x1, Pallas kernels, partial_sums(): pl.pallas_call(functools.partial(kernel, n), out_shape=jax.ShapeDtypeStru...  110 us

commit v1 on v0

v1 whole, which is shorter than its diff:
```python
import functools

import jax
import jax.numpy as jnp
from jax import lax
from jax.experimental import pallas as pl
from jax.experimental.pallas import tpu as pltpu
from jax.sharding import PartitionSpec as P

MESH = pl.DeviceIdType.MESH
F32 = jnp.float32
BF16 = jnp.bfloat16


def row_at(place, n):
    back = place // (n // 2)
    return 2 * place * (1 - back) + (2 * (n - 1 - place) + 1) * back


UNITS, SPLIT = 4, 2
RING = (3, 2, 2, 2)
PLAN = [
    ("G", 0), ("T", 1, 0), ("H", 0, 1, 0), ("T", 1, 1), ("T", 2, 0), ("T", 1, 2), ("T", 2, 1), ("G", 1),
    ("H", 0, 2, 0), ("T", 3, 0), ("T", 3, 1), ("H", 1, 1, 0), ("G", 2), ("T", 4, 0), ("H", 1, 1, 1), ("A", 1, 1),
    ("H", 1, 2, 0), ("H", 2, 1, 0), ("T", 4, 1), ("H", 0, 3, 0), ("H", 1, 2, 1), ("H", 1, 3, 0), ("A", 0, 3),
    ("H", 2, 2, 0), ("H", 2, 1, 1), ("G", 3), ("H", 0, 4, 0), ("H", 1, 3, 1), ("H", 2, 3, 0), ("A", 0, 4),
    ("H", 1, 4, 0), ("A", 1, 0), ("A", 2, 1), ("H", 2, 2, 1), ("A", 2, 2), ("A", 1, 3), ("H", 3, 1, 0), ("G", 4),
    ("A", 4, 0), ("H", 3, 1, 1), ("A", 3, 1), ("H", 1, 4, 1), ("F1", 4), ("A", 0, 2), ("H", 3, 2, 0), ("A", 3, 0),
    ("A", 2, 0), ("F2", 4), ("H", 4, 1, 0), ("A", 1, 4), ("A", 4, 1), ("A", 1, 2), ("H", 3, 2, 1), ("H", 2, 3, 1),
    ("A", 0, 1), ("A", 3, 2), ("A", 0, 0), ("H", 3, 3, 0), ("A", 2, 3), ("F1", 3), ("H", 4, 2, 0), ("F2", 3),
    ("A", 4, 2), ("H", 3, 3, 1), ("F3", 4), ("H", 2, 4, 0), ("A", 3, 3), ("H", 2, 4, 1), ("A", 2, 4), ("F1", 2),
    ("H", 3, 4, 0), ("H", 4, 3, 0), ("F2", 2), ("A", 4, 3), ("H", 3, 4, 1), ("F3", 3), ("A", 3, 4), ("F1", 1),
    ("F2", 1), ("H", 4, 4, 0), ("A", 4, 4), ("F1", 0), ("F3", 2), ("F2", 0), ("F3", 1), ("F3", 0),
]


def kernel(n, counts, tok_hbm, gate_hbm, up_hbm, down_hbm, out_ref, tok, weights, down, part, keep, theirs, hid, total, other,
           own_half, send_y, from_y, done, land, other0, half0, send0, land0, load_sem, down_send, down_recv,
           tok_send, tok_recv, y_send, y_recv, part_send, part_recv, hid_send, hid_recv, sum_send, sum_recv,
           col_send, col_recv, out_send, out_recv, last_send, last_recv):
    row, col, core = lax.axis_index("row"), lax.axis_index("col"), lax.axis_index("depth")
    half = n // 2
    x, z = row % 2, row // 2
    place = z * (1 - x) + (n - 1 - z) * x
    ways = ({"row": row_at((place + 1) % n, n)}, {"row": row_at((place + n - 1) % n, n)})
    beside, partner = {"col": 1 - col}, {"depth": 1 - core}
    block = tok_hbm.shape[0]
    units = gate_hbm.shape[0]
    share = units // 2
    features, held = down_hbm.shape
    middle = features // 2
    window = hid.shape[2]
    unit_rows = block // UNITS

    def remote(src, dst, send, recv, to):
        return pltpu.make_async_remote_copy(src_ref=src, dst_ref=dst, send_sem=send, recv_sem=recv,
                                            device_id=to, device_id_type=MESH)

    loads = [pltpu.make_async_copy(tok_hbm, tok.at[0], load_sem.at[0]),
             pltpu.make_async_copy(gate_hbm, weights.at[0], load_sem.at[1]),
             pltpu.make_async_copy(up_hbm, weights.at[1], load_sem.at[2]),
             pltpu.make_async_copy(down_hbm, down.at[:, pl.ds(0, held)], load_sem.at[3])]
    for copy in loads:
        copy.start()
    barrier = pltpu.get_barrier_semaphore()
    for peer in ways + (beside, partner):
        pl.semaphore_signal(barrier, inc=1, device_id=peer, device_id_type=MESH)
    with jax.named_scope("barrier"):
        pl.semaphore_wait(barrier, 4)
    with jax.named_scope("tokload"):
        loads[0].wait()

    def slot(hop, way):
        return 0 if hop == 0 else 1 if hop == half else 2 * hop + way

    def rounds(hop, unit):
        return (2 * unit // RING[hop - 1],) if hop == half else (0, 1)

    tok_keys, y_keys, hid_keys, whole = {}, {}, {}, []

    def number(keys, *key):
        return keys.setdefault(key, len(keys))

    def unit_at(unit, side):
        return pl.ds(pl.multiple_of(unit_rows * (unit * (1 - side) + (UNITS - 1 - unit) * side), unit_rows), unit_rows)

    def tok_copy(hop, way, unit):
        rows = unit_at(unit, col)
        return remote(tok.at[slot(hop - 1, way), rows], tok.at[slot(hop, way), rows],
                      tok_send, tok_recv.at[number(tok_keys, way, hop, unit)], ways[way])

    def y_copy(at, unit, side):
        rows = unit_at(unit, side)
        return remote(tok.at[at, rows], tok.at[at, rows], y_send, y_recv.at[number(y_keys, at, unit)], beside)

    for unit in range(RING[0]):
        for way in (0, 1):
            tok_copy(1, way, unit).start()

    def row_shift(source):
        return pl.multiple_of(source // half * 2 * (share % 128) + core * (share % 128), share % 128)

    given = down.at[:, pl.ds(held, half * window)]
    give = []
    for i in range(half):
        q = 2 * i + 1 - core
        lanes = pl.ds(pl.multiple_of(q * share // 128 * 128, 128), window)
        give.append(remote(down.at[:, lanes], down.at[:, pl.ds(held + i * window, window)],
                           down_send, down_recv, partner))

    def product(kind, which, slots):
        rows = pl.ds(pl.multiple_of(which * share, 16), share)
        seen = tok[slots[0]:slots[0] + len(slots)].reshape(block * len(slots), tok.shape[2])
        return lax.dot_general(weights[kind, rows, :], seen, (((1,), (1,)), ((), ())), preferred_element_type=F32)

    def lanes_of(piece):
        return (half - 1, 0, block) if piece == 0 else (half - 1, block, block) if piece == half else (
            piece - 1, 0, 2 * block)

    def parts_of(piece):
        return 1 if piece in (0, half) else SPLIT

    def hid_at(at, piece, source, part_of):
        index, first, wide = lanes_of(piece)
        wide = wide // parts_of(piece)
        return hid.at[at, index, pl.ds(row_shift(source), share), pl.ds(first + part_of * wide, wide)]

    def hid_sems(piece, hop, way, part_of):
        return hid_send, hid_recv.at[number(hid_keys, way, hop, piece, part_of)], ways[way]

    def hid_copy(piece, hop, way, part_of):
        source = (place + (n - hop + 1 if way == 0 else hop - 1)) % n
        return remote(hid_at(slot(hop - 1, way), piece, source, part_of), hid_at(slot(hop, way), piece, source, part_of),
                      *hid_sems(piece, hop, way, part_of))

    def hid_wait(piece, hop, way, part_of):
        source = (place + (n - hop if way == 0 else hop)) % n
        at = hid_at(slot(hop, way), piece, source, part_of)
        remote(at, at, *hid_sems(piece, hop, way, part_of)).wait_recv()

    def hid_rounds(piece, hop):
        return (piece % 2,) if hop == half else (0, 1)

    def swap(group, kind, wide):
        return remote(part.at[group, kind, :, pl.ds(0, wide)], theirs.at[group, kind, :, pl.ds(0, wide)],
                      part_send, part_recv.at[group], partner)

    def gate_up(group):
        slots = [0] if group == 0 else [1] if group == half else [2 * group, 2 * group + 1]
        wide = block * len(slots)
        if group == 0:
            loads[1].wait()
            loads[2].wait()
        else:
            for unit in range(UNITS - RING[group - 1]):
                for way in rounds(group, unit):
                    with jax.named_scope(f"ywait#g={group}#u={unit}#w={way}"):
                        y_copy(slot(group, way), unit, 1 - col).wait_recv()
        for kind in (0, 1):
            part[group, kind, :, :wide] = product(kind, 1 - core, slots)
            swap(group, kind, wide).start()
        for kind in (0, 1):
            keep[kind, :, :wide] = product(kind, core, slots)
        if group == 0:
            loads[3].wait()
            for copy in give:
                copy.start()
        with jax.named_scope(f"swapwait#g={group}"):
            both = theirs.at[group, :, :, pl.ds(0, wide)]
            remote(both, both, part_send, part_recv.at[group], partner).wait_recv()
        gate = keep[0, :, :wide] + theirs[group, 0, :, :wide]
        up = keep[1, :, :wide] + theirs[group, 1, :, :wide]
        index, first, wide = lanes_of(group)
        hid[0, index, pl.ds(row_shift(place), share), first:first + wide] = (
            gate / (1.0 + jnp.exp(-gate)) * up).astype(BF16)
        for part_of in range(parts_of(group)):
            for way in (0, 1):
                hid_copy(group, 1, way, part_of).start()

    def token_hop(hop, unit):
        for way in rounds(hop, unit):
            with jax.named_scope(f"tokwait#h={hop}#u={unit}#w={way}"):
                tok_copy(hop, way, unit).wait_recv()
            if hop < half and unit < RING[hop] and way in rounds(hop + 1, unit):
                tok_copy(hop + 1, way, unit).start()
            if unit < UNITS - RING[hop - 1]:
                y_copy(slot(hop, way), unit, col).start()

    def hid_hop(piece, hop, part_of):
        for way in hid_rounds(piece, hop):
            with jax.named_scope(f"hidwait#p={piece}#h={hop}#q={part_of}#w={way}"):
                hid_wait(piece, hop, way, part_of)
            if hop < half and way in hid_rounds(piece, hop + 1):
                hid_copy(piece, hop + 1, way, part_of).start()

    def add_one(at, source, piece):
        index, first, wide = lanes_of(piece)
        at_row = row_at(source, n)
        same = 1 - (at_row // half - core) * (at_row // half - core)
        mine = (2 * (at_row % half) + core) * share // 128 * 128
        start = pl.multiple_of(same * mine + (1 - same) * (held + at_row % half * window), 128)
        term = lax.dot_general(down[:, pl.ds(start, window)], hid[at, index, :, first:first + wide],
                               (((1,), (0,)), ((), ())), preferred_element_type=F32)
        if piece in (0, half):
            total[(source + piece) % n] += term
        else:
            for k, token_block in enumerate(((source + n - piece) % n, (source + piece) % n)):
                total[token_block] += term[:, k * block:(k + 1) * block]

    def add_down(piece, hop):
        if not whole:
            whole.append(True)
            remote(given, given, down_send, down_recv, partner).wait_recv()
        if hop == 0:
            add_one(0, place, piece)
        elif hop == half:
            add_one(1, (place + half) % n, piece)
        else:
            @pl.loop(0, 2)
            def _(way):
                add_one(2 * hop + way, (place + n - hop + 2 * hop * way) % n, piece)

    to_col, to_core = z // 2, z % 2
    near_col = 1 - (col - to_col) * (col - to_col)
    near_core = 1 - (core - to_core) * (core - to_core)

    def handled(d, by):
        return (place + half) % n if d == half else (place + d + (n - 2 * d) * by) % n

    def keep_rows(which):
        return pl.ds(pl.multiple_of(which * middle, 16), middle)

    def sum_copy(d):
        return remote(total.at[handled(d, 1 - core)], other.at[d - 1], sum_send.at[d - 1], sum_recv.at[d - 1], partner)

    def col_copy(d):
        return remote(send_y.at[d - 1], from_y.at[d - 1], col_send.at[d - 1], col_recv.at[d - 1], beside)

    def out_copy(d):
        to = {"row": row_at(handled(d, core), n), "col": to_col, "depth": to_core}
        return remote(done.at[d - 1], land.at[x, col], out_send.at[d - 1], out_recv.at[x, col], to)

    def near_copy():
        return remote(total.at[place], other0, last_send.at[0], last_recv.at[0], partner)

    def half_copy():
        return remote(total.at[place, keep_rows(1 - core)], half0, last_send.at[1], last_recv.at[1], partner)

    def far_copy():
        return remote(send0, land0.at[core], last_send.at[2], last_recv.at[2 + core], {"col": to_col, "depth": to_core})

    def only(d, who):
        return pl.when(core == who) if d == half else (lambda f: f())

    def final_1(d):
        if d:
            @only(d, 1)
            def _():
                sum_copy(d).start()
            return

        @pl.when(near_col * (1 - near_core) == 1)
        def _():
            near_copy().start()

        @pl.when(near_col == 0)
        def _():
            half_copy().start()

    def final_2(d):
        if d:
            @only(d, 0)
            def _():
                with jax.named_scope(f"sumwait#d={d}"):
                    sum_copy(d).wait_recv()
                at = handled(d, core)
                send_y[d - 1] = (total[at, keep_rows(1 - col)] + other[d - 1, keep_rows(1 - col)]).astype(BF16)
                col_copy(d).start()
                own_half[d - 1] = total[at, keep_rows(col)] + other[d - 1, keep_rows(col)]
            return

        @pl.when(near_col == 0)
        def _():
            half_copy().wait_recv()
            send0[...] = (total[place, keep_rows(core)] + half0[...]).astype(BF16)
            far_copy().start()

    def final_3(d):
        if d:
            @only(d, 0)
            def _():
                with jax.named_scope(f"colwait#d={d}"):
                    col_copy(d).wait_recv()
                done[d - 1] = (own_half[d - 1] + from_y[d - 1].astype(F32)).astype(BF16)
                out_copy(d).start()
            return

        @pl.when(near_col * near_core == 1)
        def _():
            with jax.named_scope("lastwait"):
                near_copy().wait_recv()
                for which in (0, 1):
                    remote(send0, land0.at[which], last_send.at[2], last_recv.at[2 + which], beside).wait_recv()
            for which in (0, 1):
                rows = slice(which * middle, (which + 1) * middle)
                value = total[place, rows] + other0[rows] + land0[which].astype(F32)
                out_ref[pl.ds(pl.multiple_of(x * features + which * middle, 16), middle)] = value.astype(BF16)

    total[...] = jnp.zeros_like(total)
    gap = window - share
    for at in range(n):
        hop, way = (0, 0) if at == 0 else (half, 0) if at == 1 else (at // 2, at % 2)
        shift = row_shift((place + (n - hop if way == 0 else hop)) % n)
        unit = share % 128
        for k in range(gap // unit):
            below = jnp.where(k * unit < shift, 0, share)
            rows = pl.ds(pl.multiple_of(k * unit + below, unit), unit)
            for index in range(half):
                hid[at, index, rows, :] = jnp.zeros((unit, 2 * block), BF16)

    act = {"G": gate_up, "T": token_hop, "H": hid_hop, "A": add_down, "F1": final_1, "F2": final_2, "F3": final_3}
    for name, *args in PLAN:
        with jax.named_scope(name + "_" + "_".join(map(str, args))):
            act[name](*args)

    with jax.named_scope("outwait"):
        for xx in (0, 1):
            self = near_col * near_core * (1 - (x - xx) * (x - xx))

            @pl.when(self == 0)
            def _():
                for yy in (0, 1):
                    remote(land.at[xx, yy], land.at[xx, yy], out_send.at[0], out_recv.at[xx, yy], beside).wait_recv()
                    first = xx * features + yy * middle
                    out_ref[first:first + middle] = land[xx, yy]
    with jax.named_scope("sendwait"):
        for d in range(1, half + 1):
            @only(d, 1)
            def _():
                sum_copy(d).wait_send()

            @only(d, 0)
            def _():
                col_copy(d).wait_send()
                out_copy(d).wait_send()

        @pl.when(near_col * (1 - near_core) == 1)
        def _():
            near_copy().wait_send()

        @pl.when(near_col == 0)
        def _():
            half_copy().wait_send()
            far_copy().wait_send()
        tok_sent, y_sent = tok.at[0:counts[0] // UNITS], tok.at[0:counts[1] // UNITS]
        hid_sent, part_sent = hid.at[0:n - 1, :, pl.ds(0, share)], part.at[0:half]
        for sent, sem in ((tok_sent, tok_send), (y_sent, y_send), (hid_sent, hid_send), (part_sent, part_send),
                          (given, down_send)):
            remote(sent, sent, sem, last_recv.at[0], partner).wait_send()


def fused_block(n, tokens, gate_weight, up_weight, down_weight):
    block, width = tokens.shape
    units = gate_weight.shape[0]
    held, features = down_weight.shape
    half, share = n // 2, units // 2
    window = (share + 127) // 128 * 128
    middle = features // 2
    counts = (2 * sum(RING[:-1]) + RING[-1], (n - 1) * UNITS - 2 * sum(RING[:-1]) - RING[-1],
              (n - 1) * (2 + SPLIT * (half - 1)))
    dma = pltpu.SemaphoreType.DMA
    result = pl.pallas_call(
        functools.partial(kernel, n, counts),
        out_shape=jax.ShapeDtypeStruct((2 * features, block), BF16),
        in_specs=[pl.BlockSpec(memory_space=pltpu.HBM)] * 4,
        out_specs=pl.BlockSpec(memory_space=pltpu.VMEM),
        scratch_shapes=[
            pltpu.VMEM((n, block, width), BF16),
            pltpu.VMEM((2, units, width), BF16),
            pltpu.VMEM((features, held + half * window), BF16),
            pltpu.VMEM((half + 1, 2, share, 2 * block), F32),
            pltpu.VMEM((2, share, 2 * block), F32),
            pltpu.VMEM((half + 1, 2, share, 2 * block), F32),
            pltpu.VMEM((n, half, window, 2 * block), BF16),
            pltpu.VMEM((n, features, block), F32),
            pltpu.VMEM((half, features, block), F32),
            pltpu.VMEM((half, middle, block), F32),
            pltpu.VMEM((half, middle, block), BF16),
            pltpu.VMEM((half, middle, block), BF16),
            pltpu.VMEM((half, middle, block), BF16),
            pltpu.VMEM((2, 2, middle, block), BF16),
            pltpu.VMEM((features, block), F32),
            pltpu.VMEM((middle, block), F32),
            pltpu.VMEM((middle, block), BF16),
            pltpu.VMEM((2, middle, block), BF16),
            dma((4,)), dma(()), dma(()),
            dma(()), dma((counts[0],)),
            dma(()), dma((counts[1],)),
            dma(()), dma((half + 1,)),
            dma(()), dma((counts[2],)),
            dma((half,)), dma((half,)),
            dma((half,)), dma((half,)),
            dma((half,)), dma((2, 2)),
            dma((3,)), dma((4,)),
        ],
        compiler_params=pltpu.CompilerParams(
            collective_id=0, has_side_effects=True, vmem_limit_bytes=54528 * 1024
        ),
    )(tokens, gate_weight, up_weight, down_weight.T)
    return result.T


def send_out(mine, rows, cols, depths):
    quarters = cols * depths
    per = rows // quarters
    block = mine.shape[0] // per
    width = mine.shape[1]
    row = lax.axis_index("row")
    low = row % per
    got = jnp.zeros((block, per, width), jnp.bfloat16)
    for k in range(per):
        pairs = []
        for r in range(rows):
            for q in range(quarters):
                a, e = r // per, r % per
                to_row = q * per + (e + k) % per
                pairs.append((r * quarters + q, to_row * quarters + a))
        piece = lax.dynamic_slice_in_dim(mine, (low + k) % per * block, block, 0)
        piece = lax.ppermute(piece, ("row", "col", "depth"), pairs)
        got = lax.dynamic_update_slice_in_dim(got, piece[:, None], (low - k) % per, 1)
    return got.reshape(block, per * width)


def solution(mesh):
    rows, cols, depths = (mesh.shape[a] for a in ("row", "col", "depth"))

    def local(tokens, gate_weight, up_weight, down_weight):
        units = gate_weight.shape[0]
        every = lax.all_gather(tokens, "row", axis=0, tiled=True)
        down = down_weight.reshape(rows // depths, depths, units // depths, -1)
        down = lax.all_to_all(down, "depth", split_axis=1, concat_axis=0, tiled=True)
        down = down.reshape(rows, units // depths, -1)
        paired = jnp.stack([gate_weight, up_weight])
        sums = jnp.einsum("td,gfd->gtf", every, paired, preferred_element_type=jnp.float32)
        sums = lax.psum_scatter(sums, "depth", scatter_dimension=2, tiled=True)
        hidden = (jax.nn.silu(sums[0]) * sums[1]).astype(jnp.bfloat16)
        hidden = lax.all_gather(hidden, "row", axis=0)
        partial = jnp.einsum("rtk,rkc->tc", hidden, down, preferred_element_type=jnp.float32)
        mine = lax.psum_scatter(partial, ("col", "depth"), scatter_dimension=0, tiled=True)
        return send_out(mine.astype(BF16), rows, cols, depths)

    def fused(*args):
        return fused_block(rows, *args)

    in_specs = (
        P("row", "depth"),
        P(("col", "row"), "depth"),
        P(("col", "row"), "depth"),
        P(("col", "depth"), "row"),
    )
    out_specs = P("row", ("col", "depth"))
    small = cols == 2 and depths == 2 and rows == 8
    return jax.shard_map(fused if small else local, mesh=mesh, in_specs=in_specs, out_specs=out_specs, check_vma=False)
```

time: 113 us -> 94.7 us (0.84)
  Pallas kernels: 110 us -> 93.8 us
  local copies, waits for them, and re-layouts: 1.96 us -> 0.73 us
    pallas_call x1, Pallas kernels: 110 us -> 93.8 us  [fused_block(): pl.pallas_call(functools.partial(kernel, n, counts), out_shape=jax.ShapeD...]
where the time goes in v1:
time: 94.7 us; the launch traced here: 94.6 us
  Pallas kernels  93.8 us (99%)
    pallas_call x1, Pallas kernels, fused_block(): pl.pallas_call(functools.partial(kernel, n, counts), out_shape=jax.ShapeD...  93.8 us

profile of v1, /device:TPU:0, one launch (start us, length us, event | category | flops | bytes accessed | tf_op | source)
XLA Modules:
  0.0 94.6 jit_solution(6309612341292257914)
XLA Ops:
  0.0 93.8 %shard_map.46 = bf16[1344,128]{1,0:T(8,128)(2,1)S(1)} custom-call(bf16[128,2688]{1,0:T(8,128)(2,1)} %tok_hbm.1, bf16[576,2688]{1,0:T(8,128)(2,1)} %gate_hbm.1, bf16[576,2688]{1,0:T(8,128)(2,1)} %up_hbm.1, bf16[672,2304]{1,0:T(8,128)(2,1)} %bitcast.3), custom_call_target="tpu_custom_call" | custom-call | tf_op jit(solution)/shard_map/pallas_call | solution.py:372
  93.8 0.7 copy.6

commit v2 on v1

--- a/solution.py
+++ b/solution.py
@@ -17,27 +17,39 @@
     return 2 * place * (1 - back) + (2 * (n - 1 - place) + 1) * back
 
 
-UNITS, SPLIT = 4, 2
-RING = (3, 2, 2, 2)
+UNITS = 8
+SPLIT = (1, 2, 2, 2, 2)
+RING = (5, 4, 4, 4)
 PLAN = [
-    ("G", 0), ("T", 1, 0), ("H", 0, 1, 0), ("T", 1, 1), ("T", 2, 0), ("T", 1, 2), ("T", 2, 1), ("G", 1),
-    ("H", 0, 2, 0), ("T", 3, 0), ("T", 3, 1), ("H", 1, 1, 0), ("G", 2), ("T", 4, 0), ("H", 1, 1, 1), ("A", 1, 1),
-    ("H", 1, 2, 0), ("H", 2, 1, 0), ("T", 4, 1), ("H", 0, 3, 0), ("H", 1, 2, 1), ("H", 1, 3, 0), ("A", 0, 3),
-    ("H", 2, 2, 0), ("H", 2, 1, 1), ("G", 3), ("H", 0, 4, 0), ("H", 1, 3, 1), ("H", 2, 3, 0), ("A", 0, 4),
-    ("H", 1, 4, 0), ("A", 1, 0), ("A", 2, 1), ("H", 2, 2, 1), ("A", 2, 2), ("A", 1, 3), ("H", 3, 1, 0), ("G", 4),
-    ("A", 4, 0), ("H", 3, 1, 1), ("A", 3, 1), ("H", 1, 4, 1), ("F1", 4), ("A", 0, 2), ("H", 3, 2, 0), ("A", 3, 0),
-    ("A", 2, 0), ("F2", 4), ("H", 4, 1, 0), ("A", 1, 4), ("A", 4, 1), ("A", 1, 2), ("H", 3, 2, 1), ("H", 2, 3, 1),
-    ("A", 0, 1), ("A", 3, 2), ("A", 0, 0), ("H", 3, 3, 0), ("A", 2, 3), ("F1", 3), ("H", 4, 2, 0), ("F2", 3),
-    ("A", 4, 2), ("H", 3, 3, 1), ("F3", 4), ("H", 2, 4, 0), ("A", 3, 3), ("H", 2, 4, 1), ("A", 2, 4), ("F1", 2),
-    ("H", 3, 4, 0), ("H", 4, 3, 0), ("F2", 2), ("A", 4, 3), ("H", 3, 4, 1), ("F3", 3), ("A", 3, 4), ("F1", 1),
-    ("F2", 1), ("H", 4, 4, 0), ("A", 4, 4), ("F1", 0), ("F3", 2), ("F2", 0), ("F3", 1), ("F3", 0),
+    ("G", 0), ("T", 1, 0), ("T", 1, 1), ("T", 1, 2), ("T", 2, 0), ("T", 1, 3), ("T", 2, 1), ("T", 2, 2),
+    ("T", 1, 4), ("G", 1), ("H", 0, 1, 0), ("T", 2, 3), ("T", 3, 0), ("T", 3, 1), ("H", 1, 1, 0), ("H", 0, 2, 0),
+    ("T", 3, 2), ("T", 3, 3), ("H", 1, 1, 1), ("G", 2), ("H", 1, 2, 1), ("H", 2, 1, 0), ("H", 2, 1, 1),
+    ("H", 1, 2, 0), ("T", 4, 0), ("A", 2, 0), ("A", 2, 1), ("A", 0, 1), ("T", 4, 1), ("H", 2, 2, 0), ("T", 4, 2),
+    ("H", 1, 3, 1), ("T", 4, 3), ("H", 0, 3, 0), ("G", 3), ("H", 1, 3, 0), ("H", 2, 2, 1), ("A", 1, 2),
+    ("H", 2, 3, 0), ("A", 2, 2), ("A", 0, 2), ("A", 0, 3), ("A", 0, 0), ("A", 1, 3), ("A", 3, 0), ("H", 3, 1, 0),
+    ("G", 4), ("A", 4, 0), ("H", 3, 1, 1), ("H", 0, 4, 0), ("A", 0, 4), ("A", 3, 1), ("F1", 4), ("H", 1, 4, 0),
+    ("A", 1, 1), ("H", 1, 4, 1), ("H", 3, 2, 0), ("H", 4, 1, 0), ("F2", 4), ("A", 1, 4), ("A", 1, 0),
+    ("H", 4, 1, 1), ("A", 4, 1), ("H", 3, 2, 1), ("H", 2, 3, 1), ("A", 2, 3), ("H", 2, 4, 0), ("A", 3, 2),
+    ("F1", 3), ("H", 3, 3, 0), ("F2", 3), ("H", 4, 2, 0), ("H", 4, 2, 1), ("A", 4, 2), ("H", 3, 3, 1), ("F3", 4),
+    ("A", 3, 3), ("H", 2, 4, 1), ("A", 2, 4), ("F1", 2), ("F3", 3), ("H", 4, 3, 0), ("H", 4, 3, 1), ("A", 4, 3),
+    ("F2", 2), ("H", 3, 4, 1), ("H", 3, 4, 0), ("A", 3, 4), ("F1", 1), ("F2", 1), ("H", 4, 4, 0), ("H", 4, 4, 1),
+    ("A", 4, 4), ("F3", 2), ("F1", 0), ("F2", 0), ("F3", 0),
 ]
 
 
+def box_of(rows, n, block, width):
+    total = rows * width
+    for k in range(n, 0, -1):
+        for r in range(block, 0, -16):
+            wide = total // (k * r)
+            if k * r * wide == total and wide % 128 == 0 and wide <= width:
+                return slice(0, k), pl.ds(0, r), pl.ds(0, wide)
+
+
 def kernel(n, counts, tok_hbm, gate_hbm, up_hbm, down_hbm, out_ref, tok, weights, down, part, keep, theirs, hid, total, other,
-           own_half, send_y, from_y, done, land, other0, half0, send0, land0, load_sem, down_send, down_recv,
+           own_half, send_y, from_y, done, land, direct, land1, other0, half0, send0, land0, load_sem, down_send, down_recv,
            tok_send, tok_recv, y_send, y_recv, part_send, part_recv, hid_send, hid_recv, sum_send, sum_recv,
-           col_send, col_recv, out_send, out_recv, last_send, last_recv):
+           col_send, col_recv, out_send, out_recv, last_send, last_recv, direct_recv):
     row, col, core = lax.axis_index("row"), lax.axis_index("col"), lax.axis_index("depth")
     half = n // 2
     x, z = row % 2, row // 2
@@ -118,12 +130,16 @@
             piece - 1, 0, 2 * block)
 
     def parts_of(piece):
-        return 1 if piece in (0, half) else SPLIT
+        return SPLIT[piece]
 
     def hid_at(at, piece, source, part_of):
         index, first, wide = lanes_of(piece)
-        wide = wide // parts_of(piece)
-        return hid.at[at, index, pl.ds(row_shift(source), share), pl.ds(first + part_of * wide, wide)]
+        if wide > block:
+            wide = wide // parts_of(piece)
+            return hid.at[at, index, pl.ds(row_shift(source), share), pl.ds(first + part_of * wide, wide)]
+        rows = share // parts_of(piece)
+        start = pl.multiple_of(row_shift(source) + part_of * rows, 16)
+        return hid.at[at, index, pl.ds(start, rows), pl.ds(first, wide)]
 
     def hid_sems(piece, hop, way, part_of):
         return hid_send, hid_recv.at[number(hid_keys, way, hop, piece, part_of)], ways[way]
@@ -240,6 +256,10 @@
         to = {"row": row_at(handled(d, core), n), "col": to_col, "depth": to_core}
         return remote(done.at[d - 1], land.at[x, col], out_send.at[d - 1], out_recv.at[x, col], to)
 
+    def direct_copy():
+        to = {"row": row_at(handled(1, core), n), "col": to_col, "depth": to_core}
+        return remote(direct, land1.at[x, col], last_send.at[3], direct_recv.at[x, col], to)
+
     def near_copy():
         return remote(total.at[place], other0, last_send.at[0], last_recv.at[0], partner)
 
@@ -274,6 +294,10 @@
                 with jax.named_scope(f"sumwait#d={d}"):
                     sum_copy(d).wait_recv()
                 at = handled(d, core)
+                if d == 1:
+                    direct[...] = (total[at] + other[d - 1]).astype(BF16)
+                    direct_copy().start()
+                    return
                 send_y[d - 1] = (total[at, keep_rows(1 - col)] + other[d - 1, keep_rows(1 - col)]).astype(BF16)
                 col_copy(d).start()
                 own_half[d - 1] = total[at, keep_rows(col)] + other[d - 1, keep_rows(col)]
@@ -289,6 +313,8 @@
         if d:
             @only(d, 0)
             def _():
+                if d == 1:
+                    return
                 with jax.named_scope(f"colwait#d={d}"):
                     col_copy(d).wait_recv()
                 done[d - 1] = (own_half[d - 1] + from_y[d - 1].astype(F32)).astype(BF16)
@@ -325,14 +351,23 @@
 
     with jax.named_scope("outwait"):
         for xx in (0, 1):
-            self = near_col * near_core * (1 - (x - xx) * (x - xx))
-
-            @pl.when(self == 0)
+            from_z = half // 2 * col + core
+            away = (place + n - (n - 1 - from_z if xx else from_z)) % n
+            beside_me = 1 - jnp.minimum((away - 1) * (away - 1) * (away - n + 1) * (away - n + 1), 1)
+
+            @pl.when((1 - beside_me) * away > 0)
             def _():
                 for yy in (0, 1):
                     remote(land.at[xx, yy], land.at[xx, yy], out_send.at[0], out_recv.at[xx, yy], beside).wait_recv()
                     first = xx * features + yy * middle
                     out_ref[first:first + middle] = land[xx, yy]
+
+            @pl.when(beside_me > 0)
+            def _():
+                for yy in (0, 1):
+                    remote(direct, land1.at[xx, yy], last_send.at[3], direct_recv.at[xx, yy], beside).wait_recv()
+                value = land1[xx, 0].astype(F32) + land1[xx, 1].astype(F32)
+                out_ref[xx * features:(xx + 1) * features] = value.astype(BF16)
     with jax.named_scope("sendwait"):
         for d in range(1, half + 1):
             @only(d, 1)
@@ -341,6 +376,9 @@
 
             @only(d, 0)
             def _():
+                if d == 1:
+                    direct_copy().wait_send()
+                    return
                 col_copy(d).wait_send()
                 out_copy(d).wait_send()
 
@@ -352,7 +390,7 @@
         def _():
             half_copy().wait_send()
             far_copy().wait_send()
-        tok_sent, y_sent = tok.at[0:counts[0] // UNITS], tok.at[0:counts[1] // UNITS]
+        tok_sent, y_sent = (tok.at[box_of(k * unit_rows, n, block, tok.shape[2])] for k in counts[:2])
         hid_sent, part_sent = hid.at[0:n - 1, :, pl.ds(0, share)], part.at[0:half]
         for sent, sem in ((tok_sent, tok_send), (y_sent, y_send), (hid_sent, hid_send), (part_sent, part_send),
                           (given, down_send)):
@@ -367,7 +405,7 @@
     window = (share + 127) // 128 * 128
     middle = features // 2
     counts = (2 * sum(RING[:-1]) + RING[-1], (n - 1) * UNITS - 2 * sum(RING[:-1]) - RING[-1],
-              (n - 1) * (2 + SPLIT * (half - 1)))
+              (n - 1) * sum(SPLIT))
     dma = pltpu.SemaphoreType.DMA
     result = pl.pallas_call(
         functools.partial(kernel, n, counts),
@@ -389,6 +427,8 @@
             pltpu.VMEM((half, middle, block), BF16),
             pltpu.VMEM((half, middle, block), BF16),
             pltpu.VMEM((2, 2, middle, block), BF16),
+            pltpu.VMEM((features, block), BF16),
+            pltpu.VMEM((2, 2, features, block), BF16),
             pltpu.VMEM((features, block), F32),
             pltpu.VMEM((middle, block), F32),
             pltpu.VMEM((middle, block), BF16),
@@ -401,7 +441,7 @@
             dma((half,)), dma((half,)),
             dma((half,)), dma((half,)),
             dma((half,)), dma((2, 2)),
-            dma((3,)), dma((4,)),
+            dma((4,)), dma((4,)), dma((2, 2)),
         ],
         compiler_params=pltpu.CompilerParams(
             collective_id=0, has_side_effects=True, vmem_limit_bytes=54528 * 1024

time: 94.7 us -> 91.1 us (0.962)
  Pallas kernels: 93.8 us -> 89.6 us
    pallas_call x1, Pallas kernels: 93.8 us -> 89.6 us  [fused_block(): pl.pallas_call(functools.partial(kernel, n, counts), out_shape=jax.ShapeD...]
where the time goes in v2:
time: 91.1 us; the launch traced here: 90.3 us
  Pallas kernels  89.6 us (98%)
    pallas_call x1, Pallas kernels, fused_block(): pl.pallas_call(functools.partial(kernel, n, counts), out_shape=jax.ShapeD...  89.6 us

profile of v2, /device:TPU:0, one launch (start us, length us, event | category | flops | bytes accessed | tf_op | source)
XLA Modules:
  0.0 90.3 jit_solution(9062724041236824607)
XLA Ops:
  0.0 89.6 %shard_map.46 = bf16[1344,128]{1,0:T(8,128)(2,1)S(1)} custom-call(bf16[128,2688]{1,0:T(8,128)(2,1)} %tok_hbm.1, bf16[576,2688]{1,0:T(8,128)(2,1)} %gate_hbm.1, bf16[576,2688]{1,0:T(8,128)(2,1)} %up_hbm.1, bf16[672,2304]{1,0:T(8,128)(2,1)} %bitcast.3), custom_call_target="tpu_custom_call" | custom-call | tf_op jit(solution)/shard_map/pallas_call | solution.py:410
  89.6 0.7 copy.6

commit v3 on v2

--- a/solution.py
+++ b/solution.py
@@ -17,23 +17,23 @@
     return 2 * place * (1 - back) + (2 * (n - 1 - place) + 1) * back
 
 
-UNITS = 8
+UNITS, DIRECT = 8, 1
 SPLIT = (1, 2, 2, 2, 2)
 RING = (5, 4, 4, 4)
 PLAN = [
-    ("G", 0), ("T", 1, 0), ("T", 1, 1), ("T", 1, 2), ("T", 2, 0), ("T", 1, 3), ("T", 2, 1), ("T", 2, 2),
-    ("T", 1, 4), ("G", 1), ("H", 0, 1, 0), ("T", 2, 3), ("T", 3, 0), ("T", 3, 1), ("H", 1, 1, 0), ("H", 0, 2, 0),
-    ("T", 3, 2), ("T", 3, 3), ("H", 1, 1, 1), ("G", 2), ("H", 1, 2, 1), ("H", 2, 1, 0), ("H", 2, 1, 1),
-    ("H", 1, 2, 0), ("T", 4, 0), ("A", 2, 0), ("A", 2, 1), ("A", 0, 1), ("T", 4, 1), ("H", 2, 2, 0), ("T", 4, 2),
-    ("H", 1, 3, 1), ("T", 4, 3), ("H", 0, 3, 0), ("G", 3), ("H", 1, 3, 0), ("H", 2, 2, 1), ("A", 1, 2),
-    ("H", 2, 3, 0), ("A", 2, 2), ("A", 0, 2), ("A", 0, 3), ("A", 0, 0), ("A", 1, 3), ("A", 3, 0), ("H", 3, 1, 0),
-    ("G", 4), ("A", 4, 0), ("H", 3, 1, 1), ("H", 0, 4, 0), ("A", 0, 4), ("A", 3, 1), ("F1", 4), ("H", 1, 4, 0),
-    ("A", 1, 1), ("H", 1, 4, 1), ("H", 3, 2, 0), ("H", 4, 1, 0), ("F2", 4), ("A", 1, 4), ("A", 1, 0),
-    ("H", 4, 1, 1), ("A", 4, 1), ("H", 3, 2, 1), ("H", 2, 3, 1), ("A", 2, 3), ("H", 2, 4, 0), ("A", 3, 2),
-    ("F1", 3), ("H", 3, 3, 0), ("F2", 3), ("H", 4, 2, 0), ("H", 4, 2, 1), ("A", 4, 2), ("H", 3, 3, 1), ("F3", 4),
-    ("A", 3, 3), ("H", 2, 4, 1), ("A", 2, 4), ("F1", 2), ("F3", 3), ("H", 4, 3, 0), ("H", 4, 3, 1), ("A", 4, 3),
-    ("F2", 2), ("H", 3, 4, 1), ("H", 3, 4, 0), ("A", 3, 4), ("F1", 1), ("F2", 1), ("H", 4, 4, 0), ("H", 4, 4, 1),
-    ("A", 4, 4), ("F3", 2), ("F1", 0), ("F2", 0), ("F3", 0),
+    ("T", 1, 0), ("T", 1, 1), ("T", 1, 2), ("T", 2, 0), ("T", 2, 1), ("T", 1, 3), ("G", 0), ("T", 2, 2),
+    ("T", 1, 4), ("G", 1), ("T", 2, 3), ("T", 3, 0), ("H", 1, 1, 0), ("H", 0, 1, 0), ("T", 3, 1), ("T", 3, 2),
+    ("H", 1, 1, 1), ("T", 3, 3), ("G", 2), ("H", 0, 2, 0), ("T", 4, 0), ("H", 1, 2, 0), ("H", 2, 1, 1), ("T", 4, 1),
+    ("T", 4, 2), ("H", 1, 2, 1), ("T", 4, 3), ("A", 0, 1), ("H", 2, 1, 0), ("H", 0, 3, 0), ("H", 2, 2, 1),
+    ("H", 1, 3, 0), ("G", 3), ("A", 1, 1), ("H", 1, 3, 1), ("A", 0, 0), ("H", 2, 3, 1), ("H", 2, 2, 0), ("A", 2, 2),
+    ("H", 3, 1, 0), ("G", 4), ("H", 3, 1, 1), ("A", 0, 3), ("H", 1, 4, 0), ("A", 1, 2), ("A", 0, 2), ("A", 2, 1),
+    ("H", 3, 2, 0), ("H", 0, 4, 0), ("A", 1, 0), ("A", 1, 3), ("H", 4, 1, 1), ("H", 1, 4, 1), ("A", 3, 0),
+    ("H", 4, 1, 0), ("A", 1, 4), ("A", 4, 1), ("H", 2, 4, 1), ("H", 3, 2, 1), ("H", 2, 3, 0), ("A", 2, 3),
+    ("A", 3, 1), ("H", 3, 3, 0), ("A", 3, 2), ("A", 2, 0), ("H", 4, 2, 1), ("F1", 3), ("A", 4, 0), ("H", 4, 2, 0),
+    ("A", 0, 4), ("F1", 4), ("A", 4, 2), ("F2", 3), ("H", 3, 3, 1), ("A", 3, 3), ("H", 3, 4, 0), ("H", 2, 4, 0),
+    ("F2", 4), ("A", 2, 4), ("F1", 2), ("H", 4, 3, 1), ("H", 4, 3, 0), ("F2", 2), ("A", 4, 3), ("H", 3, 4, 1),
+    ("F3", 3), ("A", 3, 4), ("F1", 1), ("H", 4, 4, 1), ("F2", 1), ("H", 4, 4, 0), ("F3", 4), ("A", 4, 4), ("F3", 2),
+    ("F1", 0), ("F2", 0), ("F3", 0),
 ]
 
 
@@ -72,7 +72,7 @@
              pltpu.make_async_copy(gate_hbm, weights.at[0], load_sem.at[1]),
              pltpu.make_async_copy(up_hbm, weights.at[1], load_sem.at[2]),
              pltpu.make_async_copy(down_hbm, down.at[:, pl.ds(0, held)], load_sem.at[3])]
-    for copy in loads:
+    for copy in loads[:3]:
         copy.start()
     barrier = pltpu.get_barrier_semaphore()
     for peer in ways + (beside, partner):
@@ -96,10 +96,20 @@
     def unit_at(unit, side):
         return pl.ds(pl.multiple_of(unit_rows * (unit * (1 - side) + (UNITS - 1 - unit) * side), unit_rows), unit_rows)
 
+    across = [1 - jnp.minimum((place % half - half // 2 + 1 - way) * (place % half - half // 2 + 1 - way), 1)
+              for way in (0, 1)]
+    last_way = [{"row": across[way] * (row + 1 - 2 * x) + (1 - across[way]) * ways[way]["row"]} for way in (0, 1)]
+
+    def via(hop, way):
+        if hop < half:
+            return slot(hop - 1, way), ways[way]
+        return across[way] * slot(1, 1 - way) + (1 - across[way]) * slot(half - 1, way), last_way[way]
+
     def tok_copy(hop, way, unit):
         rows = unit_at(unit, col)
-        return remote(tok.at[slot(hop - 1, way), rows], tok.at[slot(hop, way), rows],
-                      tok_send, tok_recv.at[number(tok_keys, way, hop, unit)], ways[way])
+        source, to = via(hop, way)
+        return remote(tok.at[source, rows], tok.at[slot(hop, way), rows],
+                      tok_send, tok_recv.at[number(tok_keys, way, hop, unit)], to)
 
     def y_copy(at, unit, side):
         rows = unit_at(unit, side)
@@ -108,6 +118,7 @@
     for unit in range(RING[0]):
         for way in (0, 1):
             tok_copy(1, way, unit).start()
+    loads[3].start()
 
     def row_shift(source):
         return pl.multiple_of(source // half * 2 * (share % 128) + core * (share % 128), share % 128)
@@ -142,11 +153,14 @@
         return hid.at[at, index, pl.ds(start, rows), pl.ds(first, wide)]
 
     def hid_sems(piece, hop, way, part_of):
-        return hid_send, hid_recv.at[number(hid_keys, way, hop, piece, part_of)], ways[way]
+        return hid_send, hid_recv.at[number(hid_keys, way, hop, piece, part_of)], via(hop, way)[1]
 
     def hid_copy(piece, hop, way, part_of):
         source = (place + (n - hop + 1 if way == 0 else hop - 1)) % n
-        return remote(hid_at(slot(hop - 1, way), piece, source, part_of), hid_at(slot(hop, way), piece, source, part_of),
+        if hop == half:
+            source = (across[way] * (place + n + 1 - 2 * way) + (1 - across[way]) * source) % n
+        held_at = via(hop, way)[0]
+        return remote(hid_at(held_at, piece, source, part_of), hid_at(slot(hop, way), piece, source, part_of),
                       *hid_sems(piece, hop, way, part_of))
 
     def hid_wait(piece, hop, way, part_of):
@@ -256,9 +270,9 @@
         to = {"row": row_at(handled(d, core), n), "col": to_col, "depth": to_core}
         return remote(done.at[d - 1], land.at[x, col], out_send.at[d - 1], out_recv.at[x, col], to)
 
-    def direct_copy():
-        to = {"row": row_at(handled(1, core), n), "col": to_col, "depth": to_core}
-        return remote(direct, land1.at[x, col], last_send.at[3], direct_recv.at[x, col], to)
+    def direct_copy(d):
+        to = {"row": row_at(handled(d, core), n), "col": to_col, "depth": to_core}
+        return remote(direct.at[d - 1], land1.at[x, col], last_send.at[2 + d], direct_recv.at[x, col], to)
 
     def near_copy():
         return remote(total.at[place], other0, last_send.at[0], last_recv.at[0], partner)
@@ -294,9 +308,9 @@
                 with jax.named_scope(f"sumwait#d={d}"):
                     sum_copy(d).wait_recv()
                 at = handled(d, core)
-                if d == 1:
-                    direct[...] = (total[at] + other[d - 1]).astype(BF16)
-                    direct_copy().start()
+                if d <= DIRECT:
+                    direct[d - 1] = (total[at] + other[d - 1]).astype(BF16)
+                    direct_copy(d).start()
                     return
                 send_y[d - 1] = (total[at, keep_rows(1 - col)] + other[d - 1, keep_rows(1 - col)]).astype(BF16)
                 col_copy(d).start()
@@ -313,7 +327,7 @@
         if d:
             @only(d, 0)
             def _():
-                if d == 1:
+                if d <= DIRECT:
                     return
                 with jax.named_scope(f"colwait#d={d}"):
                     col_copy(d).wait_recv()
@@ -353,19 +367,19 @@
         for xx in (0, 1):
             from_z = half // 2 * col + core
             away = (place + n - (n - 1 - from_z if xx else from_z)) % n
-            beside_me = 1 - jnp.minimum((away - 1) * (away - 1) * (away - n + 1) * (away - n + 1), 1)
-
-            @pl.when((1 - beside_me) * away > 0)
+            away = jnp.minimum(away, n - away)
+
+            @pl.when(away > DIRECT)
             def _():
                 for yy in (0, 1):
                     remote(land.at[xx, yy], land.at[xx, yy], out_send.at[0], out_recv.at[xx, yy], beside).wait_recv()
                     first = xx * features + yy * middle
                     out_ref[first:first + middle] = land[xx, yy]
 
-            @pl.when(beside_me > 0)
+            @pl.when(away * (DIRECT + 1 - away) > 0)
             def _():
                 for yy in (0, 1):
-                    remote(direct, land1.at[xx, yy], last_send.at[3], direct_recv.at[xx, yy], beside).wait_recv()
+                    remote(direct.at[0], land1.at[xx, yy], last_send.at[3], direct_recv.at[xx, yy], beside).wait_recv()
                 value = land1[xx, 0].astype(F32) + land1[xx, 1].astype(F32)
                 out_ref[xx * features:(xx + 1) * features] = value.astype(BF16)
     with jax.named_scope("sendwait"):
@@ -376,8 +390,8 @@
 
             @only(d, 0)
             def _():
-                if d == 1:
-                    direct_copy().wait_send()
+                if d <= DIRECT:
+                    direct_copy(d).wait_send()
                     return
                 col_copy(d).wait_send()
                 out_copy(d).wait_send()
@@ -427,7 +441,7 @@
             pltpu.VMEM((half, middle, block), BF16),
             pltpu.VMEM((half, middle, block), BF16),
             pltpu.VMEM((2, 2, middle, block), BF16),
-            pltpu.VMEM((features, block), BF16),
+            pltpu.VMEM((DIRECT, features, block), BF16),
             pltpu.VMEM((2, 2, features, block), BF16),
             pltpu.VMEM((features, block), F32),
             pltpu.VMEM((middle, block), F32),
@@ -441,7 +455,7 @@
             dma((half,)), dma((half,)),
             dma((half,)), dma((half,)),
             dma((half,)), dma((2, 2)),
-            dma((4,)), dma((4,)), dma((2, 2)),
+            dma((3 + DIRECT,)), dma((4,)), dma((2, 2)),
         ],
         compiler_params=pltpu.CompilerParams(
             collective_id=0, has_side_effects=True, vmem_limit_bytes=54528 * 1024

time: 91.1 us -> 91.1 us (level)
  no operation moved by 1% of the time
where the time goes in v3:
time: 91.1 us; the launch traced here: 91 us
  Pallas kernels  90.2 us (99%)
    pallas_call x1, Pallas kernels, fused_block(): pl.pallas_call(functools.partial(kernel, n, counts), out_shape=jax.ShapeD...  90.2 us

profile of v3, /device:TPU:0, one launch (start us, length us, event | category | flops | bytes accessed | tf_op | source)
XLA Modules:
  0.0 91.0 jit_solution(5168363146929221325)
XLA Ops:
  0.0 90.2 %shard_map.46 = bf16[1344,128]{1,0:T(8,128)(2,1)S(1)} custom-call(bf16[128,2688]{1,0:T(8,128)(2,1)} %tok_hbm.1, bf16[576,2688]{1,0:T(8,128)(2,1)} %gate_hbm.1, bf16[576,2688]{1,0:T(8,128)(2,1)} %up_hbm.1, bf16[672,2304]{1,0:T(8,128)(2,1)} %bitcast.3), custom_call_target="tpu_custom_call" | custom-call | tf_op jit(solution)/shard_map/pallas_call | solution.py:424
  90.3 0.7 copy.6
